TPU v7x, 256 devices: a whole 4x4x8 slice. The times are simulated.
256 devices in a mesh: fsdp: 64 (over y, z, core), refresh: 4 (over x).
Axes of the slice: x: 4, y: 4, z: 8, core: 2. Of those that a mesh axis runs over, the one named last changes fastest.
Arguments:
- gradient: bfloat16 [4, 192, 65536], P('refresh', None, 'fsdp'), may hold values from -6 to 6
- owner: int32 [4, 192, 1], P('refresh'), may hold values from 0 to 63; in each aligned block of 192 rows (0 to 191, 192 to 383, ..., all dimensions but the last counted through in order) at most 4 rows name the same one
- rotation: int32 [64], replicated, may hold values from 0 to 3
- left_factor: float32 [4, 256, 256, 256], P('refresh', 'fsdp'), may hold values from -1 to 8, as said below
- right_factor: float32 [4, 256, 256, 256], P('refresh', 'fsdp'), may hold values from -1 to 8, as said below
- left_basis: float32 [4, 256, 256, 256], P('refresh', 'fsdp'), may hold values from -1 to 1, as said below
- right_basis: float32 [4, 256, 256, 256], P('refresh', 'fsdp'), may hold values from -1 to 1, as said below
- moment: float32 [4, 256, 256, 256], P('refresh', 'fsdp'), may hold values from -4 to 4
- second_moment: float32 [4, 256, 256, 256], P('refresh', 'fsdp'), may hold values from 0.05 to 2
Outputs:
- direction: float32 [4, 192, 65536], P('refresh', None, 'fsdp')
- left_factor_new: float32 [4, 256, 256, 256], P('refresh', 'fsdp')
- right_factor_new: float32 [4, 256, 256, 256], P('refresh', 'fsdp')
- left_basis_new: float32 [4, 256, 256, 256], P('refresh', 'fsdp')
- right_basis_new: float32 [4, 256, 256, 256], P('refresh', 'fsdp')
- moment_new: float32 [4, 256, 256, 256], P('refresh', 'fsdp')
- second_moment_new: float32 [4, 256, 256, 256], P('refresh', 'fsdp')
Inputs may be any that keep to these rules, and one draw needn't show every extreme that they name: Within each group no owner is named by more than 4 blocks, a bound that some block reaches; some owner is named by at least one block. The state of block b lies in slot s(b) of the steps; the states of slots that no block takes are carried unchanged. `left_factor`: each slot's factor is symmetric positive definite. `right_factor`: each slot's factor is symmetric positive definite. `left_basis`: each slot's basis is orthogonal. `right_basis`: each slot's basis is orthogonal.
All inputs are finite; a program needn't handle non-finite values.
Results may differ from a plain program's by a relative error of at most 0.0003.
Values may be sent and summed in bfloat16 or wider, within the bound.
No kernel may reach another device: no remote copies, remote signals or barrier semaphores. Data moves between devices by JAX's collectives and lax.ppermute only.
A program may use at most 64 MiB of HBM per device.

v0:
```python
import jax
import jax.numpy as jnp
from jax import lax
from jax.sharding import PartitionSpec as P

HIGHEST = lax.Precision.HIGHEST
EPSILON = 1e-08


def split_up(value, dim, length):
    before, after = (value.shape[:dim], value.shape[dim + 1 :])
    return jnp.moveaxis(value.reshape(*before, length, -1, *after), dim, 0)


def sum_at_owner(value, axis, dim):
    blocks = split_up(value, dim, lax.axis_size(axis))
    arrived = lax.all_to_all(blocks, axis, split_axis=0, concat_axis=0, tiled=True)
    return arrived.sum(axis=0)


def image_of(factor, basis):
    return jnp.einsum("sij,sjk->sik", factor, basis, precision=HIGHEST)


def finish_step(image):
    gram = jnp.einsum("sji,sjk->sik", image, image, precision=HIGHEST)
    lower = jnp.linalg.cholesky(gram)
    solved = jax.scipy.linalg.solve_triangular(lower, jnp.swapaxes(image, 1, 2), lower=True)
    return jnp.swapaxes(solved, 1, 2)


def rotate_pair(left, middle, right):
    inner = jnp.einsum("sji,sjk->sik", left, middle, precision=HIGHEST)
    return jnp.einsum("sij,sjk->sik", inner, right, precision=HIGHEST)


def body(
    gradient,
    owner,
    rotation,
    left_factor,
    right_factor,
    left_basis,
    right_basis,
    moment,
    second_moment,
):
    shards = lax.axis_size("fsdp")
    helpers = lax.axis_size("refresh")
    mine = lax.axis_index("fsdp")
    group = lax.axis_index("refresh")
    cap = left_factor.shape[1]
    width = left_factor.shape[2]
    owners = owner[0, :, 0]
    onehot = (owners[:, None] == jnp.arange(shards, dtype=jnp.int32)[None, :]).astype(jnp.int32)
    before = jnp.cumsum(onehot, axis=0) - onehot
    target = owners * cap + jnp.sum(before * onehot, axis=1)
    placing = (target[None, :] == jnp.arange(shards * cap, dtype=jnp.int32)[:, None]).astype(
        jnp.bfloat16
    )
    outgoing = jnp.dot(placing, gradient[0], preferred_element_type=jnp.float32).astype(
        jnp.bfloat16
    )
    arrived = lax.all_to_all(outgoing, "fsdp", split_axis=0, concat_axis=1, tiled=True)
    blocks = arrived.reshape(cap, width, width)
    count = jnp.sum((owners == mine).astype(jnp.int32))
    keep = (jnp.arange(cap, dtype=jnp.int32) < count)[:, None, None]
    left_old = left_factor[0]
    right_old = right_factor[0]
    left_turn = left_basis[0]
    right_turn = right_basis[0]
    gram_left = jnp.einsum("sij,skj->sik", blocks, blocks, preferred_element_type=jnp.float32)
    gram_right = jnp.einsum("sji,sjk->sik", blocks, blocks, preferred_element_type=jnp.float32)
    left_new = 0.95 * left_old + 0.05 / width * gram_left
    right_new = 0.95 * right_old + 0.05 / width * gram_right
    wide = blocks.astype(jnp.float32)
    moment_next = 0.9 * moment[0] + 0.1 * wide
    turned = rotate_pair(left_turn, wide, right_turn)
    turned_moment = rotate_pair(left_turn, moment_next, right_turn)
    second_next = 0.95 * second_moment[0] + 0.05 * turned * turned
    scaled = turned_moment / (jnp.sqrt(second_next) + EPSILON)
    backed = jnp.einsum("sij,sjk->sik", left_turn, scaled, precision=HIGHEST)
    update = jnp.einsum("sij,skj->sik", backed, right_turn, precision=HIGHEST)
    returned = lax.all_to_all(
        update.reshape(cap, width * width), "fsdp", split_axis=1, concat_axis=0, tiled=True
    )
    direction = jnp.take(returned, target, axis=0)
    factors = jnp.stack([left_new[0], right_new[0]], axis=0)
    bases = jnp.stack([left_turn[0], right_turn[0]], axis=0)
    chosen = lax.dynamic_index_in_dim(rotation, mine, 0, keepdims=False)
    share_count = -(-2 // helpers)
    extra = share_count * helpers - 2
    filler = jnp.broadcast_to(jnp.eye(width, dtype=jnp.float32), (extra, width, width))
    images_all = jnp.concatenate([image_of(factors, bases), filler], axis=0)
    offered = jnp.where(group == chosen, images_all, jnp.zeros_like(images_all))
    received = sum_at_owner(offered, "refresh", 0)
    fresh = lax.all_gather(finish_step(received), "refresh", axis=0, tiled=True)[:2]
    leading = (jnp.arange(cap, dtype=jnp.int32) == 0)[:, None, None]
    refreshed = keep & leading & (group == chosen)
    left_basis_new = jnp.where(refreshed, fresh[0][None], left_turn)
    right_basis_new = jnp.where(refreshed, fresh[1][None], right_turn)
    return (
        direction[None],
        jnp.where(keep, left_new, left_old)[None],
        jnp.where(keep, right_new, right_old)[None],
        left_basis_new[None],
        right_basis_new[None],
        jnp.where(keep, moment_next, moment[0])[None],
        jnp.where(keep, second_next, second_moment[0])[None],
    )


def solution(mesh):
    in_specs = (
        P("refresh", None, "fsdp"),
        P("refresh", None, None),
        P(),
        P("refresh", "fsdp", None, None),
        P("refresh", "fsdp", None, None),
        P("refresh", "fsdp", None, None),
        P("refresh", "fsdp", None, None),
        P("refresh", "fsdp", None, None),
        P("refresh", "fsdp", None, None),
    )
    out_specs = (
        P("refresh", None, "fsdp"),
        P("refresh", "fsdp", None, None),
        P("refresh", "fsdp", None, None),
        P("refresh", "fsdp", None, None),
        P("refresh", "fsdp", None, None),
        P("refresh", "fsdp", None, None),
        P("refresh", "fsdp", None, None),
    )
    return jax.shard_map(body, mesh=mesh, in_specs=in_specs, out_specs=out_specs, check_vma=False)
```

profile of v0, /device:TPU:1, one launch (start us, length us, event | category | flops | bytes accessed | tf_op | source)
XLA Modules:
  0.0 188.3 jit_solution(3342980316965750241)
XLA Ops:
  10.2 13.3 %all-to-all-start = ((bf16[64,4,1024]{2,1,0:T(4,128)(2,1)}), bf16[64,4,1024]{2,1,0:T(4,128)(2,1)S(1)}, u32[]{:S(2)}, u32[]{:S(2)}) async-start(bf16[64,4,1024]{2,1,0:T(4,128)(2,1)} %all_to_all.29), calls=%async_computation | async-start | bytes 1048576 | tf_op jit(solution)/shard_map/all_to_all | solution.py:64
  28.9 11.9 %all-to-all-done = bf16[64,4,1024]{2,1,0:T(4,128)(2,1)S(1)} async-done(((bf16[64,4,1024]{2,1,0:T(4,128)(2,1)}), bf16[64,4,1024]{2,1,0:T(4,128)(2,1)S(1)}, u32[]{:S(2)}, u32[]{:S(2)}) %all-to-all-start) | async-done | bytes 524320 | tf_op jit(solution)/shard_map/all_to_all | solution.py:64
  43.1 2.0 %fusion.17 = f32[4,256,256]{1,2,0:T(8,128)} fusion(bf16[4,256,256]{2,1,0:T(8,128)(2,1)S(1)} %reshape.256, f32[1,4,256,256]{3,2,1,0:T(8,128)S(1)} %copy-done.1), kind=kOutput, calls=%fused_computation.33 | convolution fusion | flops 805306368 | bytes 2621440 | tf_op jit(solution)/shard_map/sji,sjk->sik/dot_general | solution.py:33
  50.2 4.4 %all-to-all-start.2 = ((f32[4,1,256,256]{3,2,1,0:T(8,128)}), f32[4,1,256,256]{3,2,1,0:T(8,128)}, u32[]{:S(2)}, u32[]{:S(2)}) async-start(f32[4,1,256,256]{3,2,1,0:T(8,128)} %fusion.4), calls=%async_computation.2 | async-start | bytes 2097152 | tf_op jit(solution)/shard_map/all_to_all | solution.py:17
  54.7 3.3 %fusion.19 = f32[4,256,256]{1,2,0:T(8,128)S(1)} fusion(f32[1,4,256,256]{3,2,1,0:T(8,128)S(1)} %copy-done.1, bf16[4,256,256]{2,1,0:T(8,128)(2,1)S(1)} %reshape.256, f32[1,4,256,256]{3,2,1,0:T(8,128)} %param.16), kind=kOutput, calls=%fused_computation.35 | convolution fusion | flops 806354944 | bytes 3670016 | tf_op jit(solution)/shard_map/sji,sjk->sik/dot_general | solution.py:33
  61.9 2.1 %fusion.8 = f32[4,256,256]{2,1,0:T(8,128)} fusion(f32[4,256,256]{1,2,0:T(8,128)S(1)} %fusion.15, f32[1,4,256,256]{3,2,1,0:T(8,128)S(1)} %copy-done.2), kind=kOutput, calls=%fused_computation.26 | convolution fusion | flops 805306368 | bytes 3145728 | tf_op jit(solution)/shard_map/sij,skj->sik/dot_general | solution.py:83
  64.0 2.5 %all_to_all.32 = f32[4,64,1024]{2,1,0:T(8,128)} reshape(f32[4,256,256]{2,1,0:T(8,128)} %fusion.8) | data formatting | bytes 2097152 | tf_op jit(solution)/shard_map/all_to_all | solution.py:84
  66.5 2.9 %copy.92 = f32[4,64,1024]{2,0,1:T(4,128)} copy(f32[4,64,1024]{2,1,0:T(8,128)} %all_to_all.32) | data formatting | bytes 2097152 | tf_op jit(solution)/shard_map/all_to_all | solution.py:84
  69.5 7.0 %all-to-all-start.1 = ((f32[4,64,1024]{2,0,1:T(4,128)}), f32[4,64,1024]{2,0,1:T(4,128)}, u32[]{:S(2)}, u32[]{:S(2)}) async-start(f32[4,64,1024]{2,0,1:T(4,128)} %copy.92), calls=%async_computation.1 | async-start | bytes 2097152 | tf_op jit(solution)/shard_map/all_to_all | solution.py:84
  80.4 11.7 %custom-call.17 = f32[1,128,128]{2,1,0:T(8,128)S(1)} custom-call(f32[1,128,128]{2,1,0:T(8,128)S(1)} %cholesky.117), custom_call_target="Cholesky" | custom-call | tf_op jit(solution)/shard_map/jit(cholesky)/cholesky | solution.py:27
  94.2 11.3 %custom-call.18 = f32[1,1,128,128]{2,3,1,0:T(8,128)} custom-call(f32[1,1,128,128]{3,2,1,0:T(8,128)} %get-tuple-element.39), custom_call_target="InvertDiagBlocksLowerTriangular" | custom-call | tf_op jit(solution)/shard_map/jit(cholesky)/cholesky | solution.py:27
  107.5 12.5 %custom-call.19 = f32[1,128,128]{2,1,0:T(8,128)S(1)} custom-call(f32[1,128,128]{2,1,0:T(8,128)} %fusion.2), custom_call_target="Cholesky" | custom-call | tf_op jit(solution)/shard_map/jit(cholesky)/cholesky | solution.py:27
  122.7 5.2 %while.1 = (s32[]{:T(128)}, f32[256,256]{1,0:T(8,128)S(1)}, s32[2,2]{1,0:T(2,128)S(1)}, f32[2,128,128]{2,1,0:T(8,128)}, s32[]{:T(128)}) while((s32[]{:T(128)}, f32[256,256]{1,0:T(8,128)S(1)}, s32[2,2]{1,0:T(2,128)S(1)}, f32[2,128,128]{2,1,0:T(8,128)}, s32[]{:T(128)}) %tuple.33), condition=%wide.while_cond, body=%wide.while_body.sunk | while | flops 2 | bytes 132205 | solution.py:28
  123.3 2.0 %bitcast_dynamic-update-slice_fusion.3 = f32[2,128,128]{2,1,0:T(8,128)} fusion(f32[2,128,128]{2,1,0:T(8,128)} %get-tuple-element.86, s32[]{:T(128)S(6)} %copy.120, f32[256,256]{1,0:T(8,128)S(1)} %get-tuple-element.89, s32[]{:T(128)} %bitcast.158, s32[]{:T(128)} %bitcast.159), kind=kLoop, calls=%fused_computation.1.clone.1 | loop fusion | bytes 132100 | tf_op jit(solution)/shard_map/jit(_solve_triangular)/triangular_solve
  125.9 2.0 %bitcast_dynamic-update-slice_fusion.3 = f32[2,128,128]{2,1,0:T(8,128)} fusion(f32[2,128,128]{2,1,0:T(8,128)} %get-tuple-element.86, s32[]{:T(128)S(6)} %copy.120, f32[256,256]{1,0:T(8,128)S(1)} %get-tuple-element.89, s32[]{:T(128)} %bitcast.158, s32[]{:T(128)} %bitcast.159), kind=kLoop, calls=%fused_computation.1.clone.1 | loop fusion | bytes 132100 | tf_op jit(solution)/shard_map/jit(_solve_triangular)/triangular_solve
  127.9 20.5 %custom-call.20 = f32[2,128,128]{1,2,0:T(8,128)S(1)} custom-call(f32[2,128,128]{2,1,0:T(8,128)} %get-tuple-element.14), custom_call_target="InvertDiagBlocksLowerTriangular" | custom-call | tf_op jit(solution)/shard_map/jit(_solve_triangular)/triangular_solve | solution.py:28
  155.9 2.5 %mul.104 = f32[1,4,256,256]{3,2,1,0:T(8,128)} reshape(f32[4,64,1024]{2,1,0:T(8,128)} %convert_multiply_fusion) | data formatting | bytes 2097152 | tf_op jit(solution)/shard_map/mul | solution.py:77
  158.3 2.9 %add_select_fusion = f32[1,4,256,256]{3,2,1,0:T(8,128)} fusion(f32[1,4,256,256]{3,2,1,0:T(8,128)} %param.16, f32[1,4,256,256]{3,2,1,0:T(8,128)} %mul.104, pred[4]{0:T(512)(128)(4,1)S(1)} %iota_compare_fusion.9), kind=kLoop, calls=%fused_computation.38 | loop fusion | flops 786432 | bytes 3145732 | tf_op jit(solution)/shard_map/jit(_where)/select_n | solution.py:108
  161.2 3.7 %fusion.7 = (f32[1,4,256,256]{3,2,1,0:T(8,128)}, f32[1,4,256,256]{3,2,1,0:T(8,128)}, f32[1,4,256,256]{3,2,1,0:T(8,128)}) fusion(f32[4,256,256]{2,1,0:T(8,128)} %copy-done.11, f32[1,4,256,256]{3,2,1,0:T(8,128)} %param.17, pred[4]{0:T(512)(128)(4,1)S(1)} %iota_compare_fusion.9, f32[4,256,256]{2,1,0:T(8,128)S(1)} %copy-done.4, ...), kind=kLoop, calls=%fused_computation.25 | loop fusion | flops 786432 | bytes 9437188 | tf_op jit(solution)/shard_map/broadcast_in_dim | solution.py:109
  164.9 1.6 all_to_all.35
  166.6 1.8 gather_fusion
  168.4 2.1 %bitcast_select_fusion.3 = f32[1,192,1024]{2,1,0:T(8,128)} fusion(f32[192,1024]{1,0:T(8,128)} %gather_fusion, pred[192]{0:T(512)(128)(4,1)S(1)} %get-tuple-element.30), kind=kLoop, calls=%fused_computation.43 | loop fusion | flops 196608 | bytes 1573056 | tf_op jit(solution)/shard_map/jit(_take)/select_n | solution.py:87
  170.5 7.6 %all-gather.2.cloned.1.call-done = f32[4,256,256]{2,1,0:T(8,128)} async-done(((f32[1,256,256]{2,1,0:T(8,128)}), f32[4,256,256]{2,1,0:T(8,128)}) %all-gather.2.cloned.1.call-update) | async-done | bytes 1048592 | tf_op jit(solution)/shard_map/all_gather | solution.py:97
  179.8 1.6 broadcast_select_fusion
  (113 shorter events, 38.5 us)
Async XLA Ops:
  7.2 1.8 copy-start
  7.2 0.7 copy-start.21
  9.2 18.2 %copy-start.1 = (f32[1,4,256,256]{3,2,1,0:T(8,128)S(1)}, f32[1,4,256,256]{3,2,1,0:T(8,128)}, u32[]{:S(2)}) copy-start(f32[1,4,256,256]{3,2,1,0:T(8,128)} %param.14) | copy-start | bytes 3145732
  10.2 17.9 %copy-start.2 = (f32[1,4,256,256]{3,2,1,0:T(8,128)S(1)}, f32[1,4,256,256]{3,2,1,0:T(8,128)}, u32[]{:S(2)}) copy-start(f32[1,4,256,256]{3,2,1,0:T(8,128)} %param.15) | copy-start | bytes 3145732
  10.2 30.6 %all-to-all-start = ((bf16[64,4,1024]{2,1,0:T(4,128)(2,1)}), bf16[64,4,1024]{2,1,0:T(4,128)(2,1)S(1)}, u32[]{:S(2)}, u32[]{:S(2)}) async-start(bf16[64,4,1024]{2,1,0:T(4,128)(2,1)} %all_to_all.29), calls=%async_computation | async-start | bytes 1048576 | tf_op jit(solution)/shard_map/all_to_all | solution.py:64
  43.1 2.0 %copy-start.7 = (f32[1,4,256,256]{3,2,1,0:T(8,128)S(1)}, f32[1,4,256,256]{3,2,1,0:T(8,128)}, u32[]{:S(2)}) copy-start(f32[1,4,256,256]{3,2,1,0:T(8,128)} %param.13) | copy-start | bytes 3145732
  45.2 1.2 copy-start.9
  45.5 1.2 copy-start.3
  46.7 2.1 %copy-start.5 = (f32[4,256,256]{2,1,0:T(8,128)}, f32[4,256,256]{2,1,0:T(8,128)S(1)}, u32[]{:S(2)}) copy-start(f32[4,256,256]{2,1,0:T(8,128)S(1)} %fusion.1) | copy-start | bytes 3145732
  46.8 1.1 copy-start.14
  46.8 1.4 copy-start.15
  48.2 0.9 copy-start.13
  50.2 19.2 %all-to-all-start.2 = ((f32[4,1,256,256]{3,2,1,0:T(8,128)}), f32[4,1,256,256]{3,2,1,0:T(8,128)}, u32[]{:S(2)}, u32[]{:S(2)}) async-start(f32[4,1,256,256]{3,2,1,0:T(8,128)} %fusion.4), calls=%async_computation.2 | async-start | bytes 2097152 | tf_op jit(solution)/shard_map/all_to_all | solution.py:17
  54.7 3.3 %copy-start.10 = (f32[1,4,256,256]{3,2,1,0:T(8,128)S(1)}, f32[1,4,256,256]{3,2,1,0:T(8,128)}, u32[]{:S(2)}) copy-start(f32[1,4,256,256]{3,2,1,0:T(8,128)} %param.17) | copy-start | bytes 3145732
  54.7 3.3 %copy-start.12 = (f32[4,256,256]{1,2,0:T(8,128)S(1)}, f32[4,256,256]{1,2,0:T(8,128)}, u32[]{:S(2)}) copy-start(f32[4,256,256]{1,2,0:T(8,128)} %fusion.17) | copy-start | bytes 3145732
  59.3 1.4 copy-start.11
  69.5 95.5 %all-to-all-start.1 = ((f32[4,64,1024]{2,0,1:T(4,128)}), f32[4,64,1024]{2,0,1:T(4,128)}, u32[]{:S(2)}, u32[]{:S(2)}) async-start(f32[4,64,1024]{2,0,1:T(4,128)} %copy.92), calls=%async_computation.1 | async-start | bytes 2097152 | tf_op jit(solution)/shard_map/all_to_all | solution.py:84
  76.5 101.7 %all-gather.2.cloned.1.call-start = ((), (), s32[]{:S(2)}) async-start(), calls=%async_computation.3 | async-start | bytes 1310720 | tf_op jit(solution)/shard_map/all_gather | solution.py:97
  79.7 0.7 copy-start.16
  80.4 25.1 %copy-start.17 = (f32[1,256,256]{2,1,0:T(8,128)S(1)}, f32[1,256,256]{2,1,0:T(8,128)}, u32[]{:S(2)}) copy-start(f32[1,256,256]{2,1,0:T(8,128)} %copy-done.16) | copy-start | bytes 786436
  150.3 1.2 copy-start.20
  158.3 2.9 %copy-start.4 = (f32[4,256,256]{2,1,0:T(8,128)S(1)}, f32[4,256,256]{2,1,0:T(8,128)}, u32[]{:S(2)}) copy-start(f32[4,256,256]{2,1,0:T(8,128)} %copy-done.3) | copy-start | bytes 3145732
  158.3 2.9 %copy-start.6 = (f32[4,256,256]{2,1,0:T(8,128)S(1)}, f32[4,256,256]{2,1,0:T(8,128)}, u32[]{:S(2)}) copy-start(f32[4,256,256]{2,1,0:T(8,128)} %copy-done.5) | copy-start | bytes 3145732
  158.3 2.9 %copy-start.8 = (f32[1,4,256,256]{3,2,1,0:T(8,128)S(1)}, f32[1,4,256,256]{3,2,1,0:T(8,128)}, u32[]{:S(2)}) copy-start(f32[1,4,256,256]{3,2,1,0:T(8,128)} %param.13) | copy-start | bytes 3145732
  (5 other events, 3.2 us)
Sparse Core Ops, SparseCore 0:
  152.9 25.2 all-gather.1
where the time goes:
time: 191 us; the launch traced here: 188 us
  other arithmetic  76.1 us (40%)
  local copies, waits for them, and re-layouts  33 us (17%)
  starting transfers between devices  24.9 us (13%)
  waiting for transfers between devices  19.7 us (10%)
  matrix products  18.1 us (9%)
  between operations  16.5 us (9%)
    another operation x6, other arithmetic, finish_step(): lower = jnp.linalg.cholesky(gram)  36.8 us
    another operation x3, other arithmetic, finish_step(): jax.scipy.linalg.solve_triangular(lower, jnp.swapaxes(image, 1, 2), lower...  21.1 us
    all_to_all x1, starting transfers between devices, body(): lax.all_to_all(outgoing, 'fsdp', split_axis=0, concat_axis=1, tiled=True)  13.3 us
    all_to_all x1, waiting for transfers between devices, body(): lax.all_to_all(outgoing, 'fsdp', split_axis=0, concat_axis=1, tiled=True)  11.9 us
    all_gather x1, waiting for transfers between devices, body(): lax.all_gather(finish_step(received), 'refresh', axis=0, tiled=True)[:2]  7.61 us
    unnamed x50, local copies, waits for them, and re-layouts  7.1 us
    all_to_all x3, local copies, waits for them, and re-layouts, body(): lax.all_to_all(update.reshape(cap, width * width), 'fsdp', split_axis=1,...  6.98 us
    all_to_all x1, starting transfers between devices, body(): lax.all_to_all(update.reshape(cap, width * width), 'fsdp', split_axis=1,...  6.97 us
  transfers between devices with their start and end apart: 4, of which 3 were waited for; matrix products, arithmetic and copies ran while one was open for 55% of the time, Pallas kernels for 0%

commit v1 on v0

v1 whole, which is shorter than its diff:
```python
import functools

import jax
import jax.numpy as jnp
from jax import lax
from jax.experimental import pallas as pl
from jax.experimental.pallas import tpu as pltpu
from jax.sharding import PartitionSpec as P

HIGHEST = lax.Precision.HIGHEST
EPSILON = 1e-08
F32 = jnp.float32
BF16 = jnp.bfloat16
PANEL = 32
SUB = 8

NN = (((1,), (0,)), ((), ()))
NT = (((1,), (1,)), ((), ()))
TN = (((0,), (0,)), ((), ()))


def mul(a, b, dims=NN):
    return lax.dot_general(a, b, dims, preferred_element_type=F32)


def split2(x):
    high = x.astype(BF16)
    return high, (x - high.astype(F32)).astype(BF16)


def split3(x):
    high = x.astype(BF16)
    rest = x - high.astype(F32)
    middle = rest.astype(BF16)
    return high, middle, (rest - middle.astype(F32)).astype(BF16)


def mul3(a, b, dims=NN):
    return mul(a[0], b[0], dims) + (mul(a[0], b[1], dims) + mul(a[1], b[0], dims))


def params(mib):
    return pltpu.CompilerParams(vmem_limit_bytes=mib * 1024 * 1024)


def cost(flops, size):
    return pl.CostEstimate(flops=flops, bytes_accessed=size, transcendentals=0)


def in_hbm(x):
    return pltpu.with_memory_space_constraint(x, pltpu.HBM)


def ranks(row):
    blocks = row.shape[1]
    down = lax.broadcasted_iota(jnp.int32, (blocks, blocks), 0)
    across = lax.broadcasted_iota(jnp.int32, (blocks, blocks), 1)
    column = jnp.sum(jnp.where(down == across, row, 0.0), axis=1, keepdims=True)
    return column, row, down, across


def place_kernel(cap, owner_ref, gradient_ref, out_ref, scratch):
    slots = scratch.shape[0] // 8
    column, row, before, after = ranks(owner_ref[...].astype(F32))
    earlier = jnp.where((column == row) & (before < after), 1.0, 0.0)
    target = row * cap + jnp.sum(earlier, axis=0, keepdims=True)
    number = lax.broadcasted_iota(jnp.int32, (slots, target.shape[1]), 0).astype(F32)
    placing = jnp.where(number == target, 1.0, 0.0).astype(BF16)
    for part in range(8):
        lanes = slice(128 * part, 128 * part + 128)
        scratch[pl.ds(part, slots, stride=8), :] = mul(placing, gradient_ref[:, lanes])
    out_ref[...] = scratch[...].astype(BF16)


def ahead_kernel(
    cap, owner_ref, left_ref, right_ref, moment_ref,
    lh_ref, ll_ref, th_ref, tl_ref, rh_ref, rl_ref, turned_ref, pick_ref,
):
    left = left_ref[0]
    lh_ref[0], ll_ref[0] = split2(left)
    flipped = split2(left.T)
    th_ref[0], tl_ref[0] = flipped
    right = split2(right_ref[0])
    rh_ref[0], rl_ref[0] = right
    inner = mul3(flipped, split2(moment_ref[0]))
    turned_ref[0] = mul3(split2(inner), right)

    @pl.when(pl.program_id(0) == 0)
    def _():
        column, row, before, after = ranks(owner_ref[...].astype(F32))
        earlier = jnp.where((column == row) & (after < before), 1.0, 0.0)
        target = column * cap + jnp.sum(earlier, axis=1, keepdims=True)
        blocks, slots = pick_ref.shape
        number = lax.broadcasted_iota(jnp.int32, (blocks, slots), 1).astype(F32)
        pick_ref[...] = jnp.where(number == target, 1.0, 0.0).astype(BF16)


def update_kernel(
    x_ref, lh_hbm, ll_hbm, th_hbm, tl_hbm, rh_hbm, rl_hbm, ahead_hbm, second_hbm, count_ref,
    block_ref, next_ref, out_ref,
    lh_ref, ll_ref, th_ref, tl_ref, rh_ref, rl_ref, ahead_ref, second_ref, scratch, arrivals,
):
    width = block_ref.shape[1]
    half = 2 * width
    pair = range(2)
    step = pl.program_id(0)
    kept = (th_hbm, tl_hbm, rh_hbm, rl_hbm, ahead_hbm, second_hbm, lh_hbm, ll_hbm)
    here = (th_ref, tl_ref, rh_ref, rl_ref, ahead_ref, second_ref, lh_ref, ll_ref)

    def copies(at):
        return [
            pltpu.make_async_copy(
                source.at[pl.ds(2 * at, 2)], target.at[pl.ds(2 * at, 2)], arrivals.at[n, at]
            )
            for n, (source, target) in enumerate(zip(kept, here))
        ]

    @pl.when(step == 0)
    def _():
        for at in range(2):
            for copy in copies(at):
                copy.start()

    wide = x_ref[...].astype(F32)
    for s in pair:
        scratch[s * half : (s + 1) * half, :] = wide[:, 8 * s : 8 * s + 8, :].reshape(half, 128)
    blocks = []
    for s in pair:
        columns = [scratch[pl.ds(s * half + h, width, stride=2), :] for h in range(2)]
        blocks.append(jnp.concatenate(columns, axis=1).astype(BF16))
        block_ref[s] = blocks[s]
    for copy in copies(step):
        copy.wait()
    slot = [2 * step + s for s in pair]
    right = [(rh_ref[slot[s]], rl_ref[slot[s]]) for s in pair]
    inner = [mul(th_ref[slot[s]], blocks[s]) + mul(tl_ref[slot[s]], blocks[s]) for s in pair]
    turned = [mul3(split2(inner[s]), right[s]) for s in pair]
    scaled = []
    for s in pair:
        second = second_ref[slot[s]]
        fresh = 0.95 * second + 0.05 * turned[s] * turned[s]
        next_ref[s] = jnp.where(slot[s] < count_ref[0], fresh, second)
        moment = 0.9 * ahead_ref[slot[s]] + 0.1 * turned[s]
        scaled.append(moment / (jnp.sqrt(fresh) + EPSILON))
    backed = [mul3((lh_ref[slot[s]], ll_ref[slot[s]]), split2(scaled[s])) for s in pair]
    update = [mul3(split2(backed[s]), right[s], NT) for s in pair]
    for s in pair:
        for h in range(2):
            scratch[pl.ds(s * half + h, width, stride=2), :] = update[s][:, 128 * h : 128 * h + 128]
    for s in pair:
        part = scratch[s * half : (s + 1) * half, :]
        out_ref[:, 8 * s : 8 * s + 8, :] = part.reshape(out_ref.shape[0], 8, 128)


def state_kernel(
    block_ref, left_ref, right_ref, moment_ref, count_ref, left_out, right_out, moment_out
):
    width = block_ref.shape[1]
    block = block_ref[0]
    live = pl.program_id(0) < count_ref[0]
    left, right, moment = left_ref[0], right_ref[0], moment_ref[0]
    left_new = 0.95 * left + 0.05 / width * mul(block, block, NT)
    right_new = 0.95 * right + 0.05 / width * mul(block, block, TN)
    left_out[0] = jnp.where(live, left_new, left)
    right_out[0] = jnp.where(live, right_new, right)
    moment_out[0] = jnp.where(live, 0.9 * moment + 0.1 * block.astype(F32), moment)


def panel_step(work, first):
    width = work.shape[0]
    lead = first // 128 * 128
    groups = PANEL // SUB
    rows = [work[first + SUB * i : first + SUB * i + SUB, lead:] for i in range(groups)]
    lanes = rows[0].shape[1]
    below = lax.broadcasted_iota(jnp.int32, (SUB, 128), 0)
    done = []
    for i in range(groups):
        at = first - lead + SUB * i
        columns = [
            [jnp.broadcast_to(rows[g][:, at + j : at + j + 1], (SUB, 128)) for g in range(i, groups)]
            for j in range(SUB)
        ]
        mine = rows[i]
        scale = jnp.zeros((SUB, 128), F32)
        factors = []
        for j in range(SUB):
            root = lax.rsqrt(jnp.broadcast_to(columns[j][0][j : j + 1, :], (SUB, 128)))
            factor = [c * root for c in columns[j]]
            factors.append(factor)
            scale = jnp.where(below == j, root, scale)
            for m in range(j + 1, SUB):
                there = jnp.broadcast_to(factor[0][m : m + 1, :], (SUB, 128))
                columns[m] = [c - f * there for c, f in zip(columns[m], factor)]
            if j + 1 < SUB:
                lower = jnp.where(below > j, factor[0] * root, 0.0)
                pivot = jnp.broadcast_to(mine[j : j + 1, :], (SUB, lanes))
                mine = mine - jnp.concatenate([lower] * (lanes // 128), axis=1) * pivot
        mine = mine * jnp.concatenate([scale] * (lanes // 128), axis=1)
        done.append(mine)
        for j in range(SUB):
            pivot = jnp.broadcast_to(mine[j : j + 1, :], (SUB, lanes))
            for g in range(i + 1, groups):
                factor = jnp.concatenate([factors[j][g - i]] * (lanes // 128), axis=1)
                rows[g] = rows[g] - factor * pivot
    solved = jnp.concatenate(done, axis=0)
    work[first : first + PANEL, width:] = solved[:, width - lead :]
    later = first + PANEL
    if later < width:
        start = later // 128 * 128
        kept = solved[:, start - lead :]
        high, middle, low = split3(kept)
        reach = width - start
        sides = [part[:, :reach] for part in (high, high, middle, high, low, middle)]
        product = mul(
            jnp.concatenate(sides, axis=0),
            jnp.concatenate([high, middle, high, low, high, middle], axis=0),
            TN,
        )
        work[later:, start:] = work[later:, start:] - product[later - start :, :]


def basis_kernel(
    left_ref, right_ref, left_basis_ref, right_basis_ref, flag_ref, left_out, right_out, one, two
):
    width = left_ref.shape[1]
    works = (one, two)
    factors = (left_ref, right_ref)
    bases = (left_basis_ref, right_basis_ref)
    outs = (left_out, right_out)

    @pl.when(pl.program_id(0) == 0)
    def _():
        for work, factor, basis in zip(works, factors, bases):
            image = lax.dot_general(factor[0], basis[0], NN, precision=HIGHEST, preferred_element_type=F32)
            flipped = image.T
            work[:, width:] = flipped
            work[:, :width] = lax.dot_general(flipped, image, NN, precision=HIGHEST, preferred_element_type=F32)
        for first in range(0, width, PANEL):
            for work in works:
                panel_step(work, first)
        for work, basis, out in zip(works, bases, outs):
            out[0] = jnp.where(flag_ref[0] > 0, work[:, width:].T, basis[0])

    @pl.when(pl.program_id(0) > 0)
    def _():
        for basis, out in zip(bases, outs):
            out[0] = basis[0]


def pick_kernel(returned_ref, pick_ref, out_ref):
    slots = pick_ref.shape[1]
    pick = pick_ref[...]
    for part in range(8):
        high, middle, low = split3(returned_ref[pl.ds(part, slots, stride=8), :])
        out_ref[:, 128 * part : 128 * part + 128] = mul(pick, high) + (mul(pick, middle) + mul(pick, low))


def body(
    gradient,
    owner,
    rotation,
    left_factor,
    right_factor,
    left_basis,
    right_basis,
    moment,
    second_moment,
):
    shards = lax.axis_size("fsdp")
    mine = lax.axis_index("fsdp")
    group = lax.axis_index("refresh")
    cap, width = left_factor.shape[1:3]
    slots = shards * cap
    blocks = gradient.shape[1]
    owners = owner.reshape(1, blocks)
    square = (cap, width, width)
    one_slot = pl.BlockSpec((1, width, width), lambda s: (s, 0, 0))
    two_slots = pl.BlockSpec((2, width, width), lambda s: (s, 0, 0))
    smem = pl.BlockSpec(memory_space=pltpu.SMEM)
    chunk = cap * 8
    cube = 2 * width**3


    outgoing = pl.pallas_call(
        functools.partial(place_kernel, cap),
        out_shape=jax.ShapeDtypeStruct((slots * 8, 128), BF16),
        scratch_shapes=[pltpu.VMEM((slots * 8, 128), F32)],
        compiler_params=params(56),
        cost_estimate=cost(2 * slots * blocks * 1024, 1 << 20),
        name="place",
    )(owners, gradient[0])
    arrived = lax.all_to_all(
        outgoing.reshape(shards, chunk, 128), "fsdp", split_axis=0, concat_axis=0, tiled=True
    )

    lh, ll, th, tl, rh, rl, ahead, pick = pl.pallas_call(
        functools.partial(ahead_kernel, cap),
        grid=(cap,),
        in_specs=[pl.BlockSpec((1, blocks), lambda s: (0, 0))] + [one_slot] * 3,
        out_specs=[one_slot] * 7 + [pl.BlockSpec((blocks, slots), lambda s: (0, 0))],
        out_shape=[jax.ShapeDtypeStruct(square, BF16)] * 6
        + [jax.ShapeDtypeStruct(square, F32), jax.ShapeDtypeStruct((blocks, slots), BF16)],
        compiler_params=params(56),
        cost_estimate=cost(cap * 6 * cube, 7 << 20),
        name="ahead",
    )(owners, left_basis[0], right_basis[0], moment[0])

    count = jnp.sum((owners == mine).astype(jnp.int32)).reshape(1)
    chosen = lax.dynamic_index_in_dim(rotation, mine, 0, keepdims=True)
    flag = ((group == chosen) & (count > 0)).astype(jnp.int32)

    pair_chunk = pl.BlockSpec((shards, chunk // 2, 128), lambda t: (0, t, 0))
    placed, second_new, update = pl.pallas_call(
        update_kernel,
        grid=(cap // 2,),
        in_specs=[pair_chunk] + [pl.BlockSpec(memory_space=pltpu.HBM)] * 8 + [smem],
        out_specs=[two_slots, two_slots, pair_chunk],
        out_shape=[
            jax.ShapeDtypeStruct(square, BF16),
            jax.ShapeDtypeStruct(square, F32),
            jax.ShapeDtypeStruct((shards, chunk, 128), F32),
        ],
        scratch_shapes=[pltpu.VMEM(square, BF16)] * 6
        + [pltpu.VMEM(square, F32)] * 2
        + [pltpu.VMEM((4 * width, 128), F32), pltpu.SemaphoreType.DMA((8, 2))],
        compiler_params=params(32),
        cost_estimate=cost(cap * 11 * cube, 8 << 20),
        name="update",
    )(arrived, *map(in_hbm, (lh, ll, th, tl, rh, rl, ahead, second_moment[0])), count)
    placed = in_hbm(placed)
    returned = lax.all_to_all(update, "fsdp", split_axis=0, concat_axis=0, tiled=True)

    left_new, right_new, moment_new = pl.pallas_call(
        state_kernel,
        grid=(cap,),
        in_specs=[one_slot] * 4 + [smem],
        out_specs=[one_slot] * 3,
        out_shape=[jax.ShapeDtypeStruct(square, F32)] * 3,
        compiler_params=params(56),
        cost_estimate=cost(cap * 8 * cube, 6 << 20),
        name="state",
    )(placed, left_factor[0], right_factor[0], moment[0], count)

    left_basis_new, right_basis_new = pl.pallas_call(
        basis_kernel,
        grid=(cap,),
        in_specs=[pl.BlockSpec((1, width, width), lambda s: (0, 0, 0))] * 2 + [one_slot] * 2 + [smem],
        out_specs=[one_slot] * 2,
        out_shape=[jax.ShapeDtypeStruct(square, F32)] * 2,
        scratch_shapes=[pltpu.VMEM((width, 2 * width), F32)] * 2,
        compiler_params=params(56),
        cost_estimate=cost(400 * cube, 4 << 20),
        name="basis",
    )(left_new, right_new, left_basis[0], right_basis[0], flag)

    direction = pl.pallas_call(
        pick_kernel,
        out_shape=jax.ShapeDtypeStruct((blocks, 1024), F32),
        compiler_params=params(24),
        cost_estimate=cost(6 * slots * blocks * 1024, 2 << 20),
        name="pick",
    )(returned.reshape(slots * 8, 128), pick)
    outs = (direction, left_new, right_new, left_basis_new, right_basis_new, moment_new, second_new)
    return tuple(out[None] for out in outs)


def solution(mesh):
    spread = P("refresh", None, "fsdp")
    state = P("refresh", "fsdp", None, None)
    in_specs = (spread, P("refresh", None, None), P()) + (state,) * 6
    out_specs = (spread,) + (state,) * 6
    return jax.shard_map(body, mesh=mesh, in_specs=in_specs, out_specs=out_specs, check_vma=False)
```

time: 191 us -> 77.7 us (0.41); the launches traced: 188 us -> 77.2 us
  other arithmetic: 76.1 us -> 0.63 us
  Pallas kernels: 0 us -> 37.5 us
  local copies, waits for them, and re-layouts: 33 us -> 2.03 us
  matrix products: 18.1 us -> 0 us
  between operations: 16.5 us -> 1.93 us
  starting transfers between devices: 24.9 us -> 19.4 us
  waiting for transfers between devices: 19.7 us -> 15.7 us
    another operation x13 -> x0, other arithmetic: 58.7 us -> none  [the longest x6 36.8 us: finish_step(): lower = jnp.linalg.cholesky(gram)]
    pallas_call x0 -> x6, Pallas kernels: none -> 37.5 us  [the longest x1 15.8 us: body(): pl.pallas_call(basis_kernel, grid=(cap,), in_specs=[pl.BlockSpec((1, widt...]
    dot_general x11 -> x0, matrix products: 13.5 us -> none  [the longest x2 5.28 us: rotate_pair(): inner = jnp.einsum('sji,sjk->sik', left, middle, precision=HIGHEST)]
    all_to_all x5 -> x0, local copies, waits for them, and re-layouts: 8.93 us -> none  [the longest x3 6.98 us: body(): lax.all_to_all(update.reshape(cap, width * width), 'fsdp', split_axis=1,...]
    select_n x5 -> x0, other arithmetic: 7.71 us -> none  [the longest x1 2.87 us: body(): jnp.where(keep, moment_next, moment[0])[None]]
    all_gather x1 -> x0, waiting for transfers between devices: 7.61 us -> none  [body(): lax.all_gather(finish_step(received), 'refresh', axis=0, tiled=True)[:2]]
    another operation x11 -> x0, local copies, waits for them, and re-layouts: 6.33 us -> none
    unnamed x50 -> x8, local copies, waits for them, and re-layouts: 7.1 us -> 1.45 us
  transfers between devices with their start and end apart: 4 -> 2, of which waited for: 3 -> 2; matrix products, arithmetic and copies ran while one was open for 55% -> 2% of each run, Pallas kernels for 0% -> 35%
where the time goes in v1:
time: 77.7 us; the launch traced here: 77.2 us
  Pallas kernels  37.5 us (48%)
  starting transfers between devices  19.4 us (25%)
  waiting for transfers between devices  15.7 us (20%)
  local copies, waits for them, and re-layouts  2.03 us (3%)
  between operations  1.93 us (2%)
    pallas_call x1, Pallas kernels, body(): pl.pallas_call(basis_kernel, grid=(cap,), in_specs=[pl.BlockSpec((1, widt...  15.8 us
    all_to_all x1, starting transfers between devices, body(): lax.all_to_all(outgoing.reshape(shards, chunk, 128), 'fsdp', split_axis=0...  13.1 us
    all_to_all x1, waiting for transfers between devices, body(): lax.all_to_all(outgoing.reshape(shards, chunk, 128), 'fsdp', split_axis=0...  10.7 us
    pallas_call x1, Pallas kernels, body(): pl.pallas_call(update_kernel, grid=(cap // 2,), in_specs=[pair_chunk] + [...  6.4 us
    all_to_all x1, starting transfers between devices, body(): lax.all_to_all(update, 'fsdp', split_axis=0, concat_axis=0, tiled=True)  6.29 us
    pallas_call x1, Pallas kernels, body(): pl.pallas_call(functools.partial(ahead_kernel, cap), grid=(cap,), in_spec...  5.89 us
    pallas_call x1, Pallas kernels, body(): pl.pallas_call(state_kernel, grid=(cap,), in_specs=[one_slot] * 4 + [smem...  5.29 us
    all_to_all x1, waiting for transfers between devices, body(): lax.all_to_all(update, 'fsdp', split_axis=0, concat_axis=0, tiled=True)  4.93 us
  transfers between devices with their start and end apart: 2, of which 2 were waited for; matrix products, arithmetic and copies ran while one was open for 2% of the time, Pallas kernels for 35%

profile of v1, /device:TPU:1, one launch (start us, length us, event | category | flops | bytes accessed | tf_op | source)
XLA Modules:
  0.0 77.2 jit_solution(15522276295557221071)
XLA Ops:
  0.6 2.4 %place.1 = bf16[2048,128]{1,0:T(8,128)(2,1)} custom-call(s32[1,192]{1,0:T(1,128)} %bitcast.31, bf16[192,1024]{1,0:T(8,128)(2,1)} %bitcast.30), custom_call_target="tpu_custom_call" | custom-call | flops 100663296 | bytes 1048576 | tf_op jit(solution)/shard_map/place/pallas_call | solution.py:284
  3.0 13.1 %all-to-all-start = ((bf16[64,32,128]{2,1,0:T(8,128)(2,1)}), bf16[64,32,128]{2,1,0:T(8,128)(2,1)S(1)}, u32[]{:S(2)}, u32[]{:S(2)}) async-start(bf16[64,32,128]{2,1,0:T(8,128)(2,1)} %bitcast.21), calls=%async_computation | async-start | bytes 1048576 | tf_op jit(solution)/shard_map/all_to_all | solution.py:292
  16.2 0.0 copy-start.2
  16.2 5.9 %ahead.1 = (bf16[4,256,256]{2,1,0:T(8,128)(2,1)}, bf16[4,256,256]{2,1,0:T(8,128)(2,1)}, bf16[4,256,256]{2,1,0:T(8,128)(2,1)}, bf16[4,256,256]{2,1,0:T(8,128)(2,1...) custom-call(s32[1,192]{1,0:T(1,128)} %bitcast.32, ...), custom_call_target="tpu_custom_call" | custom-call | flops 805306368 | bytes 7340032 | tf_op jit(solution)/shard_map/ahead/pallas_call | solution.py:296
  22.1 0.0 copy-done.2
  22.1 0.6 fusion
  22.7 10.7 %all-to-all-done.x_ref = bf16[64,32,128]{2,1,0:T(8,128)(2,1)S(1)} async-done(((bf16[64,32,128]{2,1,0:T(8,128)(2,1)}), bf16[64,32,128]{2,1,0:T(8,128)(2,1)S(1)}, u32[]{:S(2)}, u32[]{:S(2)}) %all-to-all-start) | async-done | bytes 524320 | tf_op jit(solution)/shard_map/all_to_all | solution.py:292
  33.5 6.4 %update.1 = (bf16[4,256,256]{2,1,0:T(8,128)(2,1)S(1)}, f32[4,256,256]{2,1,0:T(8,128)}, f32[64,32,128]{2,1,0:T(8,128)}) custom-call(bf16[64,32,128]{2,1,0:T(8,128)(2,1)S(1)} %all-to-all-done.x_ref, bf16[4,256,256]{2,1,0:T(8,128)(2,1)} %get-tuple-element.23.lh_hbm, bf16[4,256,256]{2,1,0:T(8,128)(2,1)} %get-tuple-element.24.ll_hbm, ...), custom_call_target="tpu_custom_call" | custom-call | flops 1476395008 | bytes 8388608 | tf_op jit(solution)/shard_map/update/pallas_call | solution.py:313
  39.9 0.0 copy-start.1
  39.9 0.8 %copy-done.1 = bf16[4,256,256]{2,1,0:T(8,128)(2,1)} copy-done((bf16[4,256,256]{2,1,0:T(8,128)(2,1)}, bf16[4,256,256]{2,1,0:T(8,128)(2,1)S(1)}, u32[]{:S(2)}) %copy-start.1) | copy-done | bytes 524312
  40.7 6.3 %all-to-all-start.1 = ((f32[64,32,128]{2,1,0:T(8,128)}), f32[64,32,128]{2,1,0:T(8,128)S(1)}, u32[]{:S(2)}, u32[]{:S(2)}) async-start(f32[64,32,128]{2,1,0:T(8,128)} %get-tuple-element.30), calls=%async_computation.1 | async-start | bytes 2097152 | tf_op jit(solution)/shard_map/all_to_all | solution.py:331
  47.5 0.0 copy-start.3
  47.5 0.6 copy-done.3
  48.2 0.6 dynamic_slice.4
  49.4 5.3 %state.1 = (f32[4,256,256]{2,1,0:T(8,128)}, f32[4,256,256]{2,1,0:T(8,128)}, f32[4,256,256]{2,1,0:T(8,128)}) custom-call(bf16[4,256,256]{2,1,0:T(8,128)(2,1)} %copy-done.1, f32[4,256,256]{2,1,0:T(8,128)} %bitcast.33, f32[4,256,256]{2,1,0:T(8,128)} %bitcast.34, f32[4,256,256]{2,1,0:T(8,128)} %bitcast.23, s32[1]{0:T(128)} %bitcast.7.count_ref), custom_call_target="tpu_custom_call" | custom-call | flops 1073741824 | bytes 6291456 | tf_op jit(solution)/shard_map/state/pallas_call | solution.py:333
  54.7 0.0 copy-start
  54.7 15.8 %basis.1 = (f32[4,256,256]{2,1,0:T(8,128)}, f32[4,256,256]{2,1,0:T(8,128)}) custom-call(f32[4,256,256]{2,1,0:T(8,128)} %get-tuple-element.33.left_ref, f32[4,256,256]{2,1,0:T(8,128)} %get-tuple-element.34.right_ref, f32[4,256,256]{2,1,0:T(8,128)} %bitcast.25, f32[4,256,256]{2,1,0:T(8,128)} %bitcast.27, s32[1]{0:T(128)S(6)} %convert_element_type.15.flag_ref), custom_call_target="tpu_custom_call" | custom-call | flops 13421772800 | bytes 4194304 | tf_op jit(solution)/shard_map/basis/pallas_call | solution.py:344
  70.6 4.9 %all-to-all-done.1 = f32[64,32,128]{2,1,0:T(8,128)S(1)} async-done(((f32[64,32,128]{2,1,0:T(8,128)}), f32[64,32,128]{2,1,0:T(8,128)S(1)}, u32[]{:S(2)}, u32[]{:S(2)}) %all-to-all-start.1) | async-done | bytes 1048608 | tf_op jit(solution)/shard_map/all_to_all | solution.py:331
  75.5 0.0 copy-done
  75.5 1.7 %pick.1 = f32[192,1024]{1,0:T(8,128)} custom-call(f32[2048,128]{1,0:T(8,128)S(1)} %bitcast.20, bf16[192,256]{1,0:T(8,128)(2,1)S(1)} %copy-done), custom_call_target="tpu_custom_call" | custom-call | flops 301989888 | bytes 2097152 | tf_op jit(solution)/shard_map/pick/pallas_call | solution.py:356
Async XLA Ops:
  3.0 30.4 %all-to-all-start = ((bf16[64,32,128]{2,1,0:T(8,128)(2,1)}), bf16[64,32,128]{2,1,0:T(8,128)(2,1)S(1)}, u32[]{:S(2)}, u32[]{:S(2)}) async-start(bf16[64,32,128]{2,1,0:T(8,128)(2,1)} %bitcast.21), calls=%async_computation | async-start | bytes 1048576 | tf_op jit(solution)/shard_map/all_to_all | solution.py:292
  16.2 5.9 %copy-start.2 = (s32[1,192,1]{1,2,0:T(1,128)S(1)}, s32[1,192,1]{1,2,0:T(1,128)}, u32[]{:S(2)}) copy-start(s32[1,192,1]{1,2,0:T(1,128)} %param.10) | copy-start | bytes 2308
  39.9 0.8 %copy-start.1 = (bf16[4,256,256]{2,1,0:T(8,128)(2,1)}, bf16[4,256,256]{2,1,0:T(8,128)(2,1)S(1)}, u32[]{:S(2)}) copy-start(bf16[4,256,256]{2,1,0:T(8,128)(2,1)S(1)} %get-tuple-element.32.block_ref) | copy-start | bytes 1572868
  40.7 34.8 %all-to-all-start.1 = ((f32[64,32,128]{2,1,0:T(8,128)}), f32[64,32,128]{2,1,0:T(8,128)S(1)}, u32[]{:S(2)}, u32[]{:S(2)}) async-start(f32[64,32,128]{2,1,0:T(8,128)} %get-tuple-element.30), calls=%async_computation.1 | async-start | bytes 2097152 | tf_op jit(solution)/shard_map/all_to_all | solution.py:331
  47.5 0.7 copy-start.3
  54.7 20.8 %copy-start = (bf16[192,256]{1,0:T(8,128)(2,1)S(1)}, bf16[192,256]{1,0:T(8,128)(2,1)}, u32[]{:S(2)}) copy-start(bf16[192,256]{1,0:T(8,128)(2,1)} %get-tuple-element.31.pick_ref) | copy-start | bytes 294916
